TPU v7x, 512 devices: a whole 4x8x8 slice. The times are simulated.
512 devices in a mesh: gx: 32 (over z, y_hi, core), gy: 16 (over y_lo, x).
Axes of the slice: x: 4, y: 8 (y_hi: 2, y_lo: 4; y = y_hi * 4 + y_lo), z: 8, core: 2. Of those that a mesh axis runs over, the one named last changes fastest.
Arguments:
- hidden70: bfloat16 [32, 8192], P('gx', 'gy'), may hold values from -6 to 6
- attn_gain: float32 [8192], P('gy'), may hold values from 0.5 to 1.5
- final_gain: float32 [8192], P('gy'), may hold values from 0.5 to 1.5
- query_weight: bfloat16 [8192, 8192], P('gy', 'gx'), may hold values from -0.0625 to 0.0625
- keyvalue_weight: bfloat16 [8192, 2048], P('gy', 'gx'), may hold values from -0.0625 to 0.0625
- out_weight: bfloat16 [8192, 8192], P('gx', 'gy'), may hold values from -0.0625 to 0.0625
- key_cache: bfloat16 [32, 256, 1024], P('gy', 'gx'), may hold values from -444 to 444
- value_cache: bfloat16 [32, 256, 1024], P('gy', 'gx'), may hold values from -6 to 6
- lengths: int32 [32], P('gy'), may hold values from 2 to 256
- head70: bfloat16 [8192, 32000], P('gy', 'gx'), may hold values from -2 to 2
- adjusted_hidden: bfloat16 [32, 4096], P('gx', 'gy'), may hold values from -4 to 4
- adjusted_gain: float32 [4096], P('gy'), may hold values from 0.5 to 1.5
- adjusted_head: bfloat16 [4096, 32000], P('gy', 'gx'), may hold values from -3 to 3
- base_hidden: bfloat16 [32, 4096], P('gx', 'gy'), may hold values from -6 to 6
- base_gain: float32 [4096], P('gy'), may hold values from 0.5 to 1.5
- base_head: bfloat16 [4096, 32000], P('gy', 'gx'), may hold values from -3 to 3
Outputs:
- log_probs: float32 [32, 32000], P('gy', 'gx')
Inputs may be any that keep to these rules, and one draw needn't show every extreme that they name: Row r has valid cache slots 0 to lengths[r] - 1 and its new token stands at position lengths[r].
All inputs are finite; a program needn't handle non-finite values.
Results may differ from a plain program's by a relative error of at most 0.00065.
Values may be sent and summed in bfloat16 or wider, within the bound.
A program may use at most 64 MiB of HBM per device.

v0:
```python
import jax
import jax.numpy as jnp
from jax import lax
from jax.sharding import PartitionSpec as P

D = 8192
HEADS = 64
KV_HEADS = 8
HEAD_DIM = 128
D7 = 4096


EPS = 1e-05
THETA = 10000.0
NEGATIVE = -1e30


def copy_for_each(x, axis):
    copies = jnp.broadcast_to(x, (lax.axis_size(axis), *x.shape))
    return lax.all_to_all(copies, axis, split_axis=0, concat_axis=0, tiled=True)


def taken_together(x, axis):
    everything = copy_for_each(x, axis)
    return jnp.sum(everything, axis=0)


def in_order(pieces, dim):
    lengths = list(pieces.shape[1:])
    lengths[dim] *= pieces.shape[0]
    return jnp.moveaxis(pieces, 0, dim).reshape(lengths)


def gather_directly(x, axis, dim):
    pieces = copy_for_each(x, axis)
    return in_order(pieces, dim)


def in_blocks(x, dim, length):
    lengths = x.shape
    pieces = x.reshape(*lengths[:dim], length, lengths[dim] // length, *lengths[dim + 1 :])
    return jnp.moveaxis(pieces, dim, 0)


def sent_and_summed(x, axis, dim):
    length = lax.axis_size(axis)
    pieces = lax.all_to_all(in_blocks(x, dim, length), axis, 0, 0, tiled=True)
    return jnp.sum(pieces.astype(jnp.float32), axis=0)


def one_gather(arrays, axis, dims):
    vector = jnp.concatenate([a.reshape(-1) for a in arrays])
    lines, at, gathered = (lax.all_gather(vector, axis), 0, [])
    for a, dim in zip(arrays, dims):
        pieces = lines[:, at : at + a.size].reshape(-1, *a.shape)
        gathered.append(in_order(pieces, dim))
        at += a.size
    return tuple(gathered)


def over_copies(x, axis):
    return copy_for_each(x, axis).max(axis=0)


def side_by_side(arrays, axis, dim, along):
    columns = [a.reshape(*a.shape[:along], -1) for a in arrays]
    both = jnp.concatenate(columns, axis=along)
    out, at, gathered = (sent_and_summed(both, axis, dim), 0, [])
    for a, column in zip(arrays, columns):
        slab = out[..., at : at + column.shape[along]]
        gathered.append(slab.reshape(*slab.shape[:along], *a.shape[along:]))
        at += column.shape[along]
    return tuple(gathered)


def in_one(arrays, axis):
    vector, at, gathered = (jnp.concatenate([a.reshape(-1) for a in arrays]), 0, [])
    subtotal = taken_together(vector, axis)
    for a in arrays:
        gathered.append(subtotal[at : at + a.size].reshape(a.shape))
        at += a.size
    return tuple(gathered)


def summed_on_arrival(x, axis, dim):
    pieces = in_blocks(x, dim, lax.axis_size(axis))
    arrived = lax.all_to_all(pieces, axis, split_axis=0, concat_axis=0, tiled=True)
    return arrived.sum(axis=0)


def gathered_once(x, axis):
    leaves = jax.tree.leaves(x)
    turns = sorted(range(len(leaves)), key=lambda k: -leaves[k].size)
    width = (1, *leaves[turns[0]].shape)[-1]
    lines = [
        jnp.pad(leaves[k].reshape(-1), (0, -leaves[k].size % width)).reshape(-1, width)
        for k in turns
    ]
    both, at, found = (copy_for_each(jnp.concatenate(lines), axis), 0, {})
    for k, line in zip(turns, lines):
        slab = both[:, at : at + len(line)].reshape(len(both), -1)
        found[k] = slab[:, : leaves[k].size].reshape(-1, *leaves[k].shape)
        at += len(line)
    numbers = iter(range(len(leaves)))
    return jax.tree.map(lambda _: found[next(numbers)], x)


def folded_in_pairs(pieces, combine):
    while len(jax.tree.leaves(pieces)[0]) > 1:
        pieces = jax.vmap(combine)(
            *(jax.tree.map(lambda part: part[side::2], pieces) for side in (0, 1))
        )
    return jax.tree.map(lambda part: part[0], pieces)


def merged(x, axis, combine):
    pieces = gathered_once(x, axis)
    return folded_in_pairs(pieces, combine)


def rotate(values, positions):
    width = values.shape[-1]
    half = width // 2
    freq = THETA ** (-(jnp.arange(half, dtype=jnp.float32) * 2.0 / width))
    angle = positions.astype(jnp.float32)[:, None] * freq[None, :]
    cosine = jnp.cos(angle)[:, None, :]
    sine = jnp.sin(angle)[:, None, :]
    first = values[..., :half]
    second = values[..., half:]
    return jnp.concatenate(
        [first * cosine - second * sine, second * cosine + first * sine], axis=-1
    )


def combine_peaks(former, latter):
    largest = jnp.maximum(former[0], latter[0])
    return (
        largest,
        former[1] * jnp.exp(former[0] - largest) + latter[1] * jnp.exp(latter[0] - largest),
    )


def body(
    hidden70,
    attn_gain,
    final_gain,
    query_weight,
    keyvalue_weight,
    out_weight,
    key_cache,
    value_cache,
    lengths,
    head70,
    adjusted_hidden,
    adjusted_gain,
    adjusted_head,
    base_hidden,
    base_gain,
    base_head,
):
    resid_in = hidden70.astype(jnp.float32)
    squares = taken_together(jnp.sum(resid_in * resid_in, axis=1), "gy")
    normed = (resid_in * lax.rsqrt(squares[:, None] / D + EPS) * attn_gain).astype(jnp.bfloat16)
    query_cols = query_weight.shape[1]
    piece = gather_directly(normed, "gx", 0)
    partial_value = jnp.concatenate(
        [
            jnp.dot(piece, query_weight, preferred_element_type=jnp.float32),
            jnp.dot(piece, keyvalue_weight, preferred_element_type=jnp.float32),
        ],
        axis=1,
    )
    linear = sent_and_summed(partial_value.astype(jnp.bfloat16), "gy", 0).astype(jnp.bfloat16)
    q_linear, kv_linear = one_gather((linear[:, :query_cols], linear[:, query_cols:]), "gx", (1, 1))
    count = q_linear.shape[0]
    kv_width = KV_HEADS * HEAD_DIM
    group = HEADS // KV_HEADS
    query = rotate(q_linear.astype(jnp.float32).reshape(count, HEADS, HEAD_DIM), lengths).astype(
        jnp.bfloat16
    )
    key_new = rotate(
        kv_linear[:, :kv_width].astype(jnp.float32).reshape(count, KV_HEADS, HEAD_DIM), lengths
    ).astype(jnp.bfloat16)
    value_new = kv_linear[:, kv_width:].reshape(count, KV_HEADS, HEAD_DIM)
    scale = HEAD_DIM ** (-0.5)
    query_four = query.reshape(count, KV_HEADS, group, HEAD_DIM)
    span = key_cache.shape[1]
    keys = key_cache.reshape(count, span, KV_HEADS, HEAD_DIM)
    values = value_cache.reshape(count, span, KV_HEADS, HEAD_DIM)
    position = lax.axis_index("gx") * span + jnp.arange(span, dtype=jnp.int32)
    valid = (position[None, :] < lengths[:, None])[:, None, None, :]
    scores = (
        jnp.einsum("rkgd,rtkd->rkgt", query_four, keys, preferred_element_type=jnp.float32) * scale
    )
    scores = jnp.where(valid, scores, NEGATIVE)
    fresh_score = (
        jnp.einsum("rkgd,rkd->rkg", query_four, key_new, preferred_element_type=jnp.float32) * scale
    )
    owner = lax.axis_index("gx") == 0
    local_max = jnp.max(scores, axis=-1)
    local_max = jnp.where(owner, jnp.maximum(local_max, fresh_score), local_max)
    weights = jnp.where(valid, jnp.exp(scores - local_max[..., None]), 0.0)
    fresh = jnp.where(owner, jnp.exp(fresh_score - local_max), 0.0)
    total = jnp.sum(weights, axis=-1) + fresh
    summed = jnp.einsum(
        "rkgt,rtkd->rkgd", weights.astype(jnp.bfloat16), values, preferred_element_type=jnp.float32
    )
    summed = (
        summed
        + fresh.astype(jnp.bfloat16).astype(jnp.float32)[..., None]
        * value_new.astype(jnp.float32)[:, :, None, :]
    )
    local_heads = HEADS // lax.axis_size("gx")
    head_top = over_copies(local_max, "gx")
    factor = jnp.exp(local_max - head_top)
    scaled_sum = (summed * factor[..., None]).reshape(count, HEADS, HEAD_DIM)
    scaled_total = (total * factor).reshape(count, HEADS)
    share_sum, share_total = side_by_side(
        (scaled_sum.astype(jnp.bfloat16), scaled_total.astype(jnp.bfloat16)), "gx", 1, 2
    )
    attn = (
        (share_sum / share_total[..., None])
        .reshape(count, local_heads * HEAD_DIM)
        .astype(jnp.bfloat16)
    )
    mixed = jnp.dot(gather_directly(attn, "gy", 0), out_weight, preferred_element_type=jnp.float32)
    resid = resid_in + sent_and_summed(mixed.astype(jnp.bfloat16), "gx", 0)
    adjusted_in = adjusted_hidden.astype(jnp.float32)
    base_in = base_hidden.astype(jnp.float32)
    sum_resid, sum_adjusted, sum_base = in_one(
        (
            jnp.sum(resid * resid, axis=1),
            jnp.sum(adjusted_in * adjusted_in, axis=1),
            jnp.sum(base_in * base_in, axis=1),
        ),
        "gy",
    )
    final = (resid * lax.rsqrt(sum_resid[:, None] / D + EPS) * final_gain).astype(jnp.bfloat16)
    adjusted = (adjusted_in * lax.rsqrt(sum_adjusted[:, None] / D7 + EPS) * adjusted_gain).astype(
        jnp.bfloat16
    )
    base = (base_in * lax.rsqrt(sum_base[:, None] / D7 + EPS) * base_gain).astype(jnp.bfloat16)
    joined = jnp.concatenate([final, adjusted, base], axis=1)
    width_large = final.shape[1]
    width_small = adjusted.shape[1]
    piece = gather_directly(joined, "gx", 0)
    first = jnp.dot(piece[:, :width_large], head70, preferred_element_type=jnp.float32)
    second = jnp.dot(
        piece[:, width_large : width_large + width_small],
        adjusted_head,
        preferred_element_type=jnp.float32,
    )
    third = jnp.dot(
        piece[:, width_large + width_small :], base_head, preferred_element_type=jnp.float32
    )
    terms = first + second - third
    logits = summed_on_arrival(terms, "gy", 0)
    local_peak = jnp.max(logits, axis=1)
    local_total = jnp.sum(jnp.exp(logits - local_peak[:, None]), axis=1)
    peak, row_total = merged((local_peak, local_total), "gx", combine_peaks)
    return logits - (peak + jnp.log(row_total))[:, None]


def solution(mesh):
    placed = (
        P("gx", "gy"),
        P("gy"),
        P("gy"),
        P("gy", "gx"),
        P("gy", "gx"),
        P("gx", "gy"),
        P("gy", "gx", None),
        P("gy", "gx", None),
        P("gy"),
        P("gy", "gx"),
        P("gx", "gy"),
        P("gy"),
        P("gy", "gx"),
        P("gx", "gy"),
        P("gy"),
        P("gy", "gx"),
    )
    return jax.shard_map(body, mesh=mesh, in_specs=placed, out_specs=P("gy", "gx"), check_vma=False)
```

profile of v0, /device:TPU:1, one launch (start us, length us, event | category | flops | bytes accessed | tf_op | source)
XLA Modules:
  0.0 246.8 jit_solution(6353079353349307682)
XLA Ops:
  0.0 1.5 multiply_reduce_fusion.1
  1.5 1.3 broadcast_in_dim.77
  2.8 8.0 %all-to-all-start = ((f32[16,1,1]{2,1,0:T(1,128)}), f32[16,1,1]{2,1,0:T(1,128)S(1)}, u32[]{:S(2)}, u32[]{:S(2)}) async-start(f32[16,1,1]{2,1,0:T(1,128)} %broadcast_in_dim.77), calls=%async_computation | async-start | bytes 16384 | tf_op jit(solution)/shard_map/all_to_all | solution.py:20
  10.8 0.6 copy-done.16
  11.5 5.9 %all-to-all-done = f32[16,1,1]{2,1,0:T(1,128)S(1)} async-done(((f32[16,1,1]{2,1,0:T(1,128)}), f32[16,1,1]{2,1,0:T(1,128)S(1)}, u32[]{:S(2)}, u32[]{:S(2)}) %all-to-all-start) | async-done | bytes 96 | tf_op jit(solution)/shard_map/all_to_all | solution.py:20
  17.5 0.6 reduce_sum.120
  18.8 0.6 copy-done.10
  19.5 0.5 broadcast.87
  20.0 0.8 reduce.18
  20.9 0.6 reshape.277
  21.5 15.1 %all-to-all-start.1 = ((bf16[32,2,256]{2,1,0:T(2,128)(2,1)}), bf16[32,2,256]{2,1,0:T(2,128)(2,1)S(1)}, u32[]{:S(2)}, u32[]{:S(2)}) async-start(bf16[32,2,256]{2,1,0:T(2,128)(2,1)} %reshape.277), calls=%async_computation.1 | async-start | bytes 65536 | tf_op jit(solution)/shard_map/all_to_all | solution.py:20
  36.6 12.0 %all-to-all-done.1 = bf16[32,2,256]{2,1,0:T(2,128)(2,1)S(1)} async-done(((bf16[32,2,256]{2,1,0:T(2,128)(2,1)}), bf16[32,2,256]{2,1,0:T(2,128)(2,1)S(1)}, u32[]{:S(2)}, u32[]{:S(2)}) %all-to-all-start.1) | async-done | bytes 32800 | tf_op jit(solution)/shard_map/all_to_all | solution.py:20
  48.7 0.2 reduce.10
  48.9 0.1 convolution_convert_fusion.1
  49.1 0.7 copy-done.5
  49.9 0.6 copy.68
  50.5 3.5 %all-to-all-start.2 = ((bf16[16,2,320]{2,1,0:T(2,128)(2,1)}), bf16[16,2,320]{2,1,0:T(2,128)(2,1)S(1)}, u32[]{:S(2)}, u32[]{:S(2)}) async-start(bf16[16,2,320]{2,1,0:T(2,128)(2,1)} %copy.68), calls=%async_computation.2 | async-start | bytes 49152 | tf_op jit(solution)/shard_map/all_to_all | solution.py:47
  54.1 6.8 %all-to-all-done.2 = bf16[16,2,320]{2,1,0:T(2,128)(2,1)S(1)} async-done(((bf16[16,2,320]{2,1,0:T(2,128)(2,1)}), bf16[16,2,320]{2,1,0:T(2,128)(2,1)S(1)}, u32[]{:S(2)}, u32[]{:S(2)}) %all-to-all-start.2) | async-done | bytes 20512 | tf_op jit(solution)/shard_map/all_to_all | solution.py:47
  61.0 0.5 copy-done.8
  61.5 0.6 slice-done
  62.3 48.5 %all-gather.1 = bf16[32,1,640]{2,1,0:T(2,128)(2,1)S(1)} all-gather(bf16[1,1,640]{2,1,0:T(2,128)(2,1)S(1)} %reshape.264), channel_id=2, replica_groups=mesh['gx'=32,'gy'=16] {'gx'}, dimensions={0}, use_global_device_ids=true | all-gather | bytes 42240 | tf_op jit(solution)/shard_map/all_gather | solution.py:53
  111.4 0.2 fusion.22
  111.6 0.6 copy-done.7
  112.1 0.2 fusion.33
  112.4 0.8 reshape.279
  113.2 6.8 %all-to-all-start.3 = ((f32[32,1,128]{2,1,0:T(1,128)}), f32[32,1,128]{2,1,0:T(1,128)S(1)}, u32[]{:S(2)}, u32[]{:S(2)}) async-start(f32[32,1,128]{2,1,0:T(1,128)} %reshape.279), calls=%async_computation.3 | async-start | bytes 32768 | tf_op jit(solution)/shard_map/all_to_all | solution.py:20
  120.1 11.6 %all-to-all-done.3 = f32[32,1,128]{2,1,0:T(1,128)S(1)} async-done(((f32[32,1,128]{2,1,0:T(1,128)}), f32[32,1,128]{2,1,0:T(1,128)S(1)}, u32[]{:S(2)}, u32[]{:S(2)}) %all-to-all-start.3) | async-done | bytes 16416 | tf_op jit(solution)/shard_map/all_to_all | solution.py:20
  131.8 0.5 broadcast.88
  132.3 0.7 reduce.19
  133.0 0.2 reshape.280
  133.3 0.5 copy.74
  133.8 0.2 copy-done.15
  133.9 0.4 fusion.2
  134.4 15.3 %all_to_all.57 = bf16[32,2,2,129]{3,2,1,0:T(2,128)(2,1)S(1)} all-to-all(bf16[32,2,2,129]{3,2,1,0:T(2,128)(2,1)S(1)} %maximum_bitcast_fusion), channel_id=1, replica_groups=mesh['gx'=32,'gy'=16] {'gx'}, dimensions={0} | all-to-all | bytes 66048 | tf_op jit(solution)/shard_map/all_to_all | solution.py:47
  150.0 0.6 broadcast_in_dim.84
  150.6 3.6 %all-to-all-start.5 = ((bf16[16,2,256]{2,1,0:T(2,128)(2,1)}), bf16[16,2,256]{2,1,0:T(2,128)(2,1)S(1)}, u32[]{:S(2)}, u32[]{:S(2)}) async-start(bf16[16,2,256]{2,1,0:T(2,128)(2,1)} %broadcast_in_dim.84), calls=%async_computation.5 | async-start | bytes 32768 | tf_op jit(solution)/shard_map/all_to_all | solution.py:20
  154.2 0.7 multiply_reduce_fusion.3
  154.9 6.1 %all-to-all-done.5 = bf16[16,2,256]{2,1,0:T(2,128)(2,1)S(1)} async-done(((bf16[16,2,256]{2,1,0:T(2,128)(2,1)}), bf16[16,2,256]{2,1,0:T(2,128)(2,1)S(1)}, u32[]{:S(2)}, u32[]{:S(2)}) %all-to-all-start.5) | async-done | bytes 16416 | tf_op jit(solution)/shard_map/all_to_all | solution.py:20
  161.1 0.1 fusion.3
  161.2 0.7 reduce.20
  161.9 0.6 reshape.281
  162.5 5.2 %all-to-all-start.6 = ((bf16[32,2,256]{2,1,0:T(2,128)(2,1)}), bf16[32,2,256]{2,1,0:T(2,128)(2,1)S(1)}, u32[]{:S(2)}, u32[]{:S(2)}) async-start(bf16[32,2,256]{2,1,0:T(2,128)(2,1)} %reshape.281), calls=%async_computation.6 | async-start | bytes 65536 | tf_op jit(solution)/shard_map/all_to_all | solution.py:47
  167.7 0.6 multiply_reduce_fusion.2
  168.3 11.5 %all-to-all-done.6 = bf16[32,2,256]{2,1,0:T(2,128)(2,1)S(1)} async-done(((bf16[32,2,256]{2,1,0:T(2,128)(2,1)}), bf16[32,2,256]{2,1,0:T(2,128)(2,1)S(1)}, u32[]{:S(2)}, u32[]{:S(2)}) %all-to-all-start.6) | async-done | bytes 32800 | tf_op jit(solution)/shard_map/all_to_all | solution.py:47
  180.0 0.7 multiply_reduce_fusion
  180.6 2.0 pad_maximum_fusion.6
  182.7 9.4 %all_to_all.58 = f32[16,1,3]{2,1,0:T(1,128)S(1)} all-to-all(f32[16,1,3]{2,1,0:T(1,128)S(1)} %broadcast_in_dim.85), channel_id=1, replica_groups=mesh['gx'=32,'gy'=16] {'gy'}, dimensions={0} | all-to-all | bytes 384 | tf_op jit(solution)/shard_map/all_to_all | solution.py:20
  192.1 0.7 fusion.32
  194.7 0.7 copy-done.9
  195.4 0.7 copy-done.11
  196.1 0.7 copy-done.14
  196.9 1.0 reduce.21
  197.9 16.3 %all_to_all.59 = bf16[32,2,512]{2,1,0:T(2,128)(2,1)S(1)} all-to-all(bf16[32,2,512]{2,1,0:T(2,128)(2,1)S(1)} %reshape.283), channel_id=1, replica_groups=mesh['gx'=32,'gy'=16] {'gx'}, dimensions={0} | all-to-all | bytes 131072 | tf_op jit(solution)/shard_map/all_to_all | solution.py:20
  214.4 0.4 fusion.11
  214.8 0.6 copy-done.1
  215.4 0.3 convolution_add_fusion
  215.7 0.8 copy-done.2
  216.4 0.3 convolution_subtract_fusion
  216.8 10.4 %all_to_all.60 = f32[16,2,1000]{2,1,0:T(2,128)S(1)} all-to-all(f32[16,2,1000]{2,1,0:T(2,128)S(1)} %reshape.253), channel_id=1, replica_groups=mesh['gx'=32,'gy'=16] {'gy'}, dimensions={0} | all-to-all | bytes 256000 | tf_op jit(solution)/shard_map/all_to_all | solution.py:87
  227.2 0.1 reduce_max.29
  227.3 0.2 exponential_reduce_fusion
  227.5 16.6 %all_to_all.61 = f32[32,2,2]{2,1,0:T(2,128)S(1)} all-to-all(f32[32,2,2]{2,1,0:T(2,128)S(1)} %broadcast_in_dim.90), channel_id=1, replica_groups=mesh['gx'=32,'gy'=16] {'gx'}, dimensions={0} | all-to-all | bytes 1024 | tf_op jit(solution)/shard_map/all_to_all | solution.py:20
  246.0 0.2 add_reduce_fusion
  246.2 0.7 broadcast_subtract_fusion
  (106 shorter events, 4.2 us)
Async XLA Ops:
  0.0 214.3 %copy-start = (bf16[512,1000]{0,1:T(8,128)(2,1)S(1)}, bf16[512,1000]{0,1:T(8,128)(2,1)}, u32[]{:S(2)}) copy-start(bf16[512,1000]{0,1:T(8,128)(2,1)} %param.25) | copy-start | bytes 3072004
  2.8 14.7 %all-to-all-start = ((f32[16,1,1]{2,1,0:T(1,128)}), f32[16,1,1]{2,1,0:T(1,128)S(1)}, u32[]{:S(2)}, u32[]{:S(2)}) async-start(f32[16,1,1]{2,1,0:T(1,128)} %broadcast_in_dim.77), calls=%async_computation | async-start | bytes 16384 | tf_op jit(solution)/shard_map/all_to_all | solution.py:20
  10.8 0.7 copy-start.16
  18.7 0.7 copy-start.10
  18.7 0.7 copy-start.6
  19.5 29.4 %copy-start.3 = (bf16[512,256]{1,0:T(8,128)(2,1)S(1)}, bf16[512,256]{1,0:T(8,128)(2,1)}, u32[]{:S(2)}) copy-start(bf16[512,256]{1,0:T(8,128)(2,1)} %param.19) | copy-start | bytes 786436
  21.5 27.2 %all-to-all-start.1 = ((bf16[32,2,256]{2,1,0:T(2,128)(2,1)}), bf16[32,2,256]{2,1,0:T(2,128)(2,1)S(1)}, u32[]{:S(2)}, u32[]{:S(2)}) async-start(bf16[32,2,256]{2,1,0:T(2,128)(2,1)} %reshape.277), calls=%async_computation.1 | async-start | bytes 65536 | tf_op jit(solution)/shard_map/all_to_all | solution.py:20
  48.9 0.8 copy-start.5
  50.5 10.4 %all-to-all-start.2 = ((bf16[16,2,320]{2,1,0:T(2,128)(2,1)}), bf16[16,2,320]{2,1,0:T(2,128)(2,1)S(1)}, u32[]{:S(2)}, u32[]{:S(2)}) async-start(bf16[16,2,320]{2,1,0:T(2,128)(2,1)} %copy.68), calls=%async_computation.2 | async-start | bytes 49152 | tf_op jit(solution)/shard_map/all_to_all | solution.py:47
  61.0 0.6 copy-start.8
  61.5 0.7 slice-start
  111.4 0.8 copy-start.7
  113.2 18.6 %all-to-all-start.3 = ((f32[32,1,128]{2,1,0:T(1,128)}), f32[32,1,128]{2,1,0:T(1,128)S(1)}, u32[]{:S(2)}, u32[]{:S(2)}) async-start(f32[32,1,128]{2,1,0:T(1,128)} %reshape.279), calls=%async_computation.3 | async-start | bytes 32768 | tf_op jit(solution)/shard_map/all_to_all | solution.py:20
  133.2 0.8 copy-start.15
  134.3 26.7 %copy-start.4 = (bf16[256,512]{1,0:T(8,128)(2,1)S(1)}, bf16[256,512]{1,0:T(8,128)(2,1)}, u32[]{:S(2)}) copy-start(bf16[256,512]{1,0:T(8,128)(2,1)} %param.21) | copy-start | bytes 786436
  150.6 3.6 %copy-start.13 = (bf16[1,256]{1,0:T(2,128)(2,1)S(1)}, bf16[1,256]{1,0:T(2,128)(2,1)}, u32[]{:S(2)}) copy-start(bf16[1,256]{1,0:T(2,128)(2,1)} %param.26) | copy-start | bytes 1540
  150.6 10.5 %all-to-all-start.5 = ((bf16[16,2,256]{2,1,0:T(2,128)(2,1)}), bf16[16,2,256]{2,1,0:T(2,128)(2,1)S(1)}, u32[]{:S(2)}, u32[]{:S(2)}) async-start(bf16[16,2,256]{2,1,0:T(2,128)(2,1)} %broadcast_in_dim.84), calls=%async_computation.5 | async-start | bytes 32768 | tf_op jit(solution)/shard_map/all_to_all | solution.py:20
  162.5 5.2 %copy-start.12 = (bf16[1,256]{1,0:T(2,128)(2,1)S(1)}, bf16[1,256]{1,0:T(2,128)(2,1)}, u32[]{:S(2)}) copy-start(bf16[1,256]{1,0:T(2,128)(2,1)} %param.29) | copy-start | bytes 1540
  162.5 17.4 %all-to-all-start.6 = ((bf16[32,2,256]{2,1,0:T(2,128)(2,1)}), bf16[32,2,256]{2,1,0:T(2,128)(2,1)S(1)}, u32[]{:S(2)}, u32[]{:S(2)}) async-start(bf16[32,2,256]{2,1,0:T(2,128)(2,1)} %reshape.281), calls=%async_computation.6 | async-start | bytes 65536 | tf_op jit(solution)/shard_map/all_to_all | solution.py:47
  194.7 0.7 copy-start.9
  195.4 0.7 copy-start.11
  196.1 0.7 copy-start.14
  214.3 1.0 copy-start.1
  215.4 1.0 copy-start.2
where the time goes:
time: 248 us; the launch traced here: 247 us
  blocking collectives  116 us (47%)
  waiting for transfers between devices  54.1 us (22%)
  starting transfers between devices  42.3 us (17%)
  local copies, waits for them, and re-layouts  16.9 us (7%)
  other arithmetic  11.8 us (5%)
  between operations  3.13 us (1%)
    all_gather x1, blocking collectives, one_gather(): lines, at, gathered = (lax.all_gather(vector, axis), 0, [])  48.5 us
    all_to_all x3, blocking collectives, copy_for_each(): return lax.all_to_all(copies, axis, split_axis=0, concat_axis=0, tiled=True)  42.3 us
    all_to_all x4, waiting for transfers between devices, copy_for_each(): return lax.all_to_all(copies, axis, split_axis=0, concat_axis=0, tiled=True)  35.7 us
    all_to_all x4, starting transfers between devices, copy_for_each(): return lax.all_to_all(copies, axis, split_axis=0, concat_axis=0, tiled=True)  33.6 us
    all_to_all x2, waiting for transfers between devices, sent_and_summed(): pieces = lax.all_to_all(in_blocks(x, dim, length), axis, 0, 0, tiled=True)  18.4 us
    all_to_all x1, blocking collectives, sent_and_summed(): pieces = lax.all_to_all(in_blocks(x, dim, length), axis, 0, 0, tiled=True)  15.3 us
    all_to_all x1, blocking collectives, summed_on_arrival(): lax.all_to_all(pieces, axis, split_axis=0, concat_axis=0, tiled=True)  10.4 us
    unnamed x48, local copies, waits for them, and re-layouts  9.05 us
  transfers between devices with their start and end apart: 6, of which 6 were waited for; matrix products, arithmetic and copies ran while one was open for 1% of the time, Pallas kernels for 0%

commit v1 on v0

v1 whole, which is shorter than its diff:
```python
import functools
import math

import jax
import jax.numpy as jnp
from jax import lax
from jax.experimental import pallas as pl
from jax.experimental.pallas import tpu as pltpu
from jax.sharding import PartitionSpec as P

D = 8192
HEADS = 64
KV_HEADS = 8
HEAD_DIM = 128
D7 = 4096
CTX = 256

EPS = 1e-05
THETA = 10000.0
NEGATIVE = -1e30

GX = 32
GY = 16
MESH = pl.DeviceIdType.MESH
BF = jnp.bfloat16
F32 = jnp.float32


def times_transposed(a, b):
    return lax.dot_general(a, b, (((1,), (1,)), ((), ())), preferred_element_type=F32)


def kernel(
    lengths,
    hidden,
    attn_gain,
    final_gain,
    query_weight,
    keyvalue_weight,
    out_weight,
    key_cache,
    value_cache,
    head70,
    adjusted_hidden,
    adjusted_gain,
    adjusted_head,
    base_hidden,
    base_gain,
    base_head,
    out,
    hid_v,
    ag_v,
    fg_v,
    qw_v,
    kvw_v,
    ow_v,
    kv_v,
    h70_v,
    ah_v,
    agn_v,
    ahead_v,
    bh_v,
    bgn_v,
    bhead_v,
    x_send,
    x_recv,
    st_send,
    st_recv,
    cache_recv,
    ab_send,
    ab_recv,
    q_send,
    q_recv,
    kn_send,
    kn_recv,
    e_send,
    e_recv,
    f_send,
    f_recv,
    h_send,
    h_recv,
    abl_send,
    abl_recv,
    i_send,
    i_recv,
    j_send,
    j_recv,
    load_sem,
    send_sem,
    recv_sem,
    entered,
):
    gx = lax.axis_index("gx")
    gy = lax.axis_index("gy")
    z = gx // 4
    yh = (gx // 2) % 2
    core = gx % 2
    row = 2 * gy + yh

    pairs = [
        (hidden, hid_v),
        (adjusted_hidden, ah_v),
        (base_hidden, bh_v),
        (adjusted_gain, agn_v),
        (base_gain, bgn_v),
        (attn_gain, ag_v),
        (key_cache, kv_v.at[0]),
        (value_cache, kv_v.at[1]),
        (query_weight, qw_v),
        (keyvalue_weight, kvw_v),
        (out_weight, ow_v),
        (adjusted_head, ahead_v),
        (base_head, bhead_v),
        (final_gain, fg_v),
        (head70, h70_v),
    ]
    loads = [
        pltpu.make_async_copy(src, dst, load_sem.at[n]) for n, (src, dst) in enumerate(pairs)
    ]
    for load in loads:
        load.start()
    own_cache = [
        pltpu.make_async_copy(
            src.at[yh, :, pl.ds(pl.multiple_of(z * HEAD_DIM, HEAD_DIM), HEAD_DIM)],
            cache_recv.at[gx, n],
            load_sem.at[len(pairs) + n],
        )
        for n, src in enumerate((key_cache, value_cache))
    ]
    for load in own_cache:
        load.start()

    def over_gx(act):
        lax.fori_loop(1, GX, lambda k, c: (act(lax.rem(gx + k, GX)), c)[1], 0)

    def over_gy(act):
        lax.fori_loop(1, GY, lambda k, c: (act(lax.rem(gy + k, GY)), c)[1], 0)

    def send(n, src, dst, to):
        pltpu.make_async_remote_copy(
            src_ref=src,
            dst_ref=dst,
            send_sem=send_sem.at[n],
            recv_sem=recv_sem.at[n],
            device_id=to,
            device_id_type=MESH,
        ).start()

    def arrived(n, ref):
        pltpu.make_async_copy(ref, ref, recv_sem.at[n]).wait()

    def sent(n, ref):
        pltpu.make_async_copy(ref, ref, send_sem.at[n]).wait()

    barrier = pltpu.get_barrier_semaphore()
    over_gx(
        lambda t: pl.semaphore_signal(barrier, inc=1, device_id=(t, gy), device_id_type=MESH)
    )
    over_gy(
        lambda t: pl.semaphore_signal(barrier, inc=1, device_id=(gx, t), device_id_type=MESH)
    )

    def as_tiles(x, width):
        return [x[:, n * 128 : (n + 1) * 128] for n in range(width // 128)]

    loads[0].wait()
    own_x = jnp.concatenate(as_tiles(hid_v[...].astype(F32), 512), axis=0)
    x_send[...] = own_x.astype(BF)
    x_recv[gx] = x_send[...]
    loads[1].wait()
    loads[2].wait()
    adjusted_in = ah_v[...].astype(F32)
    base_in = bh_v[...].astype(F32)
    sum_adjusted = jnp.sum(adjusted_in * adjusted_in, axis=1, keepdims=True)
    sum_base = jnp.sum(base_in * base_in, axis=1, keepdims=True)
    st_send[...] = jnp.concatenate(
        [jnp.broadcast_to(sum_adjusted, (1, 128)), jnp.broadcast_to(sum_base, (1, 128))], axis=0
    )
    st_recv[gy] = st_send[...]

    pl.semaphore_wait(barrier, GX - 1 + GY - 1)

    over_gx(lambda t: send(0, x_send, x_recv.at[gx], (t, gy)))
    over_gy(
        lambda t: pl.semaphore_signal(entered, inc=1, device_id=(gx, t), device_id_type=MESH)
    )
    over_gy(lambda t: send(1, st_send, st_recv.at[gy], (gx, t)))
    loads[6].wait()
    loads[7].wait()

    def send_cache(t):
        head = pl.multiple_of((t // 4) * HEAD_DIM, HEAD_DIM)
        send(
            2,
            kv_v.at[:, (t // 2) % 2, :, pl.ds(head, HEAD_DIM)],
            cache_recv.at[gx],
            (t, gy),
        )

    over_gx(send_cache)

    lane = lax.broadcasted_iota(jnp.int32, (1, HEAD_DIM), 1)
    half = HEAD_DIM // 2
    pair = (lane % half).astype(F32)
    freq = jnp.exp(pair * (-2.0 / HEAD_DIM * math.log(THETA)))
    length = lengths[yh]
    angle = length.astype(F32) * freq
    cosine = jnp.cos(angle)
    sine = jnp.where(lane < half, -jnp.sin(angle), jnp.sin(angle))

    loads[5].wait()
    loads[8].wait()
    loads[9].wait()

    def from_tiles(x):
        return jnp.concatenate([x[:, n, :] for n in range(4)], axis=1)

    arrived(0, x_recv.at[pl.ds(0, GX - 1)])
    rows = from_tiles(x_recv[...].astype(F32))
    squares = jnp.sum(rows * rows, axis=1, keepdims=True)
    scaled = (rows * ag_v[...]).astype(BF)
    part_q = jnp.dot(scaled, qw_v[...], preferred_element_type=F32)
    part_kv = times_transposed(scaled, kvw_v[...])
    high = squares.astype(BF).astype(F32)
    low = squares - high
    pieces = [
        part_q[:, :128],
        part_q[:, 128:],
        jnp.broadcast_to(high, (GX, 128)),
        jnp.broadcast_to(low, (GX, 128)),
    ]
    q_send[...] = jnp.concatenate([p.reshape(GX, 1, 128) for p in pieces], axis=1).astype(BF)
    nothing = jnp.zeros_like(part_kv)
    wide = jnp.where(
        core == 0,
        jnp.concatenate([part_kv, nothing], axis=1),
        jnp.concatenate([nothing, part_kv], axis=1),
    )
    kn_send[...] = wide.reshape(GX, 1, 128)
    q_recv[row] = q_send[row]

    pl.semaphore_wait(entered, GY - 1)

    def send_q(k, c):
        r = lax.rem(row + k, GX)
        send(3, q_send.at[r], q_recv.at[row], (4 * z + 2 * (r % 2) + core, r // 2))
        return c

    lax.fori_loop(1, GX, send_q, 0)
    kind = z // 4
    head_to = (2 * z + yh) % KV_HEADS
    meets_itself = head_to == z
    slot = (kind * 2 + core) * GY + gy

    def send_kn(k, c):
        r = k // 2
        to = 4 * head_to + 2 * (r % 2) + k % 2
        itself = jnp.logical_and(to == gx, r // 2 == gy)

        @pl.when(itself)
        def _():
            kn_recv[slot] = kn_send[r]

        @pl.when(jnp.logical_not(itself))
        def _():
            send(4, kn_send.at[r], kn_recv.at[slot], (to, r // 2))

        return c

    lax.fori_loop(0, 2 * GX, send_kn, 0)

    def without_own(act):
        @pl.when(meets_itself)
        def _():
            act(4, kn_recv.at[pl.ds(0, 4 * GY - 1)])

        @pl.when(jnp.logical_not(meets_itself))
        def _():
            act(4, kn_recv)

    arrived(1, st_recv.at[pl.ds(0, GY - 1)])
    totals = jnp.sum(st_recv[...], axis=0)
    loads[3].wait()
    loads[4].wait()
    adjusted = adjusted_in * lax.rsqrt(totals[0:1, 0:1] / D7 + EPS) * agn_v[...]
    base = base_in * lax.rsqrt(totals[1:2, 0:1] / D7 + EPS) * bgn_v[...]
    ab_send[...] = jnp.concatenate(as_tiles(adjusted, 256) + as_tiles(base, 256), axis=0).astype(BF)
    ab_recv[gx] = ab_send[...]
    over_gx(lambda t: send(5, ab_send, ab_recv.at[gx], (t, gy)))

    for load in own_cache:
        load.wait()
    arrived(2, cache_recv.at[pl.ds(0, GX - 1)])
    cached = cache_recv[...].astype(F32)
    keys = cached[:, 0].reshape(CTX, HEAD_DIM).astype(BF)
    values = cached[:, 1].reshape(CTX, HEAD_DIM).astype(BF)

    arrived(3, q_recv.at[pl.ds(0, GX - 1)])
    without_own(arrived)

    q_total = jnp.zeros((2, 4, 128), F32)
    for n in range(GY):
        q_total = q_total + q_recv[2 * n : 2 * n + 2].astype(F32)
    square = q_total[0, 2:3, :] + q_total[0, 3:4, :]
    factor = lax.rsqrt(square / D + EPS)
    query = jnp.concatenate([q_total[0, 0:2, :], q_total[1, 0:2, :]], axis=0) * factor
    query = query.astype(BF).astype(F32)
    fresh_kv = kn_recv[...]
    key_new = (jnp.sum(fresh_kv[: 2 * GY], axis=0) * factor).astype(BF).astype(F32)
    value_new = (jnp.sum(fresh_kv[2 * GY :], axis=0) * factor).astype(BF).astype(F32)
    scale = HEAD_DIM ** (-0.5)
    fresh_score = jnp.sum(query * key_new, axis=1, keepdims=True) * scale
    turned = (query * cosine + pltpu.roll(query, half, 1) * sine).astype(BF)
    scores = times_transposed(turned, keys) * scale
    position = lax.broadcasted_iota(jnp.int32, (4, CTX), 1)
    valid = position < length
    scores = jnp.where(valid, scores, NEGATIVE)
    top = jnp.maximum(jnp.max(scores, axis=1, keepdims=True), fresh_score)
    weights = jnp.where(valid, jnp.exp(scores - top), 0.0)
    fresh = jnp.exp(fresh_score - top)
    total = jnp.sum(weights, axis=1, keepdims=True) + fresh
    summed = jnp.dot(weights.astype(BF), values, preferred_element_type=F32)
    summed = summed + fresh.astype(BF).astype(F32) * value_new
    attn = (summed / total).astype(BF)
    e_send[0] = attn[0:2]
    e_send[1] = attn[2:4]
    e_recv[row] = e_send[yh]

    def send_e(k, c):
        r = lax.rem(row + k, GX)
        to = r % 2
        send(6, e_send.at[to], e_recv.at[row], (4 * z + 2 * to + core, r // 2))
        return c

    lax.fori_loop(1, GX, send_e, 0)

    arrived(5, ab_recv.at[pl.ds(0, GX - 1)])
    joined = from_tiles(ab_recv[...].astype(F32)).astype(BF)
    loads[11].wait()
    loads[12].wait()
    part_ab = times_transposed(joined[:, :256], ahead_v[...]) - times_transposed(
        joined[:, 256:], bhead_v[...]
    )
    vocab = part_ab.shape[1]
    for n in range(GY):
        abl_send[n] = part_ab[2 * n : 2 * n + 2]
    abl_recv[gy] = abl_send[gy]
    over_gy(lambda t: send(7, abl_send.at[t], abl_recv.at[gy], (gx, t)))

    loads[10].wait()
    arrived(6, e_recv.at[pl.ds(0, GX - 1)])
    heads = e_recv[...].astype(F32)
    heads = jnp.concatenate([heads[:, 0, :], heads[:, 1, :]], axis=1).astype(BF)
    mixed = jnp.dot(heads, ow_v[...], preferred_element_type=F32)
    f_send[...] = jnp.concatenate(
        [p.reshape(GX, 1, 128) for p in as_tiles(mixed, 512)], axis=1
    ).astype(BF)
    f_recv[gx] = f_send[gx]

    over_gx(lambda t: send(8, f_send.at[t], f_recv.at[gx], (t, gy)))
    arrived(7, abl_recv.at[pl.ds(0, GY - 1)])
    ab_logits = jnp.sum(abl_recv[...], axis=0)
    loads[13].wait()
    loads[14].wait()
    arrived(8, f_recv.at[pl.ds(0, GX - 1)])
    resid = own_x + jnp.sum(f_recv[...].astype(F32), axis=0)

    h_send[...] = resid.astype(BF)
    h_recv[gx] = h_send[...]
    over_gx(lambda t: send(9, h_send, h_recv.at[gx], (t, gy)))
    arrived(9, h_recv.at[pl.ds(0, GX - 1)])
    rows = from_tiles(h_recv[...].astype(F32))
    squares = jnp.sum(rows * rows, axis=1, keepdims=True)
    scaled = (rows * fg_v[...]).astype(BF)
    part = times_transposed(scaled, h70_v[...])
    square = jnp.broadcast_to(squares, (GX, 128))
    for n in range(GY):
        i_send[n, :, :vocab] = part[2 * n : 2 * n + 2]
        i_send[n, :, 1024:] = square[2 * n : 2 * n + 2]
    i_recv[gy] = i_send[gy]

    over_gy(lambda t: send(10, i_send.at[t], i_recv.at[gy], (gx, t)))
    arrived(10, i_recv.at[pl.ds(0, GY - 1)])
    summed = jnp.sum(i_recv[...], axis=0)
    factor = lax.rsqrt(summed[:, 1024:1025] / D + EPS)
    logits = summed[:, :vocab] * factor + ab_logits
    peak = jnp.max(logits, axis=1, keepdims=True)
    partial_lse = peak + jnp.log(jnp.sum(jnp.exp(logits - peak), axis=1, keepdims=True))
    j_send[...] = jnp.broadcast_to(partial_lse, (2, 128))
    j_recv[gx] = j_send[...]

    over_gx(lambda t: send(11, j_send, j_recv.at[gx], (t, gy)))
    arrived(11, j_recv.at[pl.ds(0, GX - 1)])
    everyone = j_recv[...]
    peak = jnp.max(everyone, axis=0)
    lse = peak + jnp.log(jnp.sum(jnp.exp(everyone - peak[None]), axis=0))
    out[...] = logits - lse[:, 0:1]

    sent(0, x_recv.at[pl.ds(0, GX - 1)])
    sent(1, st_recv.at[pl.ds(0, GY - 1)])
    sent(2, cache_recv.at[pl.ds(0, GX - 1)])
    sent(3, q_recv.at[pl.ds(0, GX - 1)])
    without_own(sent)
    sent(5, ab_recv.at[pl.ds(0, GX - 1)])
    sent(6, e_recv.at[pl.ds(0, GX - 1)])
    sent(7, abl_recv.at[pl.ds(0, GY - 1)])
    sent(8, f_recv.at[pl.ds(0, GX - 1)])
    sent(9, h_recv.at[pl.ds(0, GX - 1)])
    sent(10, i_recv.at[pl.ds(0, GY - 1)])
    sent(11, j_recv.at[pl.ds(0, GX - 1)])


def body(
    hidden70,
    attn_gain,
    final_gain,
    query_weight,
    keyvalue_weight,
    out_weight,
    key_cache,
    value_cache,
    lengths,
    head70,
    adjusted_hidden,
    adjusted_gain,
    adjusted_head,
    base_hidden,
    base_gain,
    base_head,
):
    vocab = head70.shape[1]
    operands = (
        hidden70,
        attn_gain.reshape(1, -1),
        final_gain.reshape(1, -1),
        query_weight,
        keyvalue_weight.T,
        out_weight,
        key_cache,
        value_cache,
        head70.T,
        adjusted_hidden,
        adjusted_gain.reshape(1, -1),
        adjusted_head.T,
        base_hidden,
        base_gain.reshape(1, -1),
        base_head.T,
    )

    def like(a):
        return pltpu.VMEM(a.shape, a.dtype)

    caches = pltpu.VMEM((2, *key_cache.shape), BF)
    local = [like(a) for a in operands[:6]] + [caches] + [like(a) for a in operands[8:]]
    exchange = [
        pltpu.VMEM((4, 128), BF),
        pltpu.VMEM((GX, 4, 128), BF),
        pltpu.VMEM((2, 128), F32),
        pltpu.VMEM((GY, 2, 128), F32),
        pltpu.VMEM((GX, 2, 8, 128), BF),
        pltpu.VMEM((4, 128), BF),
        pltpu.VMEM((GX, 4, 128), BF),
        pltpu.VMEM((GX, 4, 128), BF),
        pltpu.VMEM((GX, 4, 128), BF),
        pltpu.VMEM((GX, 1, 128), F32),
        pltpu.VMEM((4 * GY, 1, 128), F32),
        pltpu.VMEM((2, 2, 128), BF),
        pltpu.VMEM((GX, 2, 128), BF),
        pltpu.VMEM((GX, 4, 128), BF),
        pltpu.VMEM((GX, 4, 128), BF),
        pltpu.VMEM((4, 128), BF),
        pltpu.VMEM((GX, 4, 128), BF),
        pltpu.VMEM((GY, 2, vocab), F32),
        pltpu.VMEM((GY, 2, vocab), F32),
        pltpu.VMEM((GY, 2, 1024 + 128), F32),
        pltpu.VMEM((GY, 2, 1024 + 128), F32),
        pltpu.VMEM((2, 128), F32),
        pltpu.VMEM((GX, 2, 128), F32),
    ]
    return pl.pallas_call(
        kernel,
        out_shape=jax.ShapeDtypeStruct((2, vocab), F32),
        in_specs=[pl.BlockSpec(memory_space=pltpu.SMEM)]
        + [pl.BlockSpec(memory_space=pl.ANY)] * len(operands),
        out_specs=pl.BlockSpec(memory_space=pltpu.VMEM),
        scratch_shapes=local
        + exchange
        + [
            pltpu.SemaphoreType.DMA((17,)),
            pltpu.SemaphoreType.DMA((12,)),
            pltpu.SemaphoreType.DMA((12,)),
            pltpu.SemaphoreType.REGULAR,
        ],
        compiler_params=pltpu.CompilerParams(collective_id=0, has_side_effects=True),
    )(lengths, *operands)


def solution(mesh):
    placed = (
        P("gx", "gy"),
        P("gy"),
        P("gy"),
        P("gy", "gx"),
        P("gy", "gx"),
        P("gx", "gy"),
        P("gy", "gx", None),
        P("gy", "gx", None),
        P("gy"),
        P("gy", "gx"),
        P("gx", "gy"),
        P("gy"),
        P("gy", "gx"),
        P("gx", "gy"),
        P("gy"),
        P("gy", "gx"),
    )
    return jax.shard_map(body, mesh=mesh, in_specs=placed, out_specs=P("gy", "gx"), check_vma=False)
```

time: 248 us -> 70.6 us (0.28)
  blocking collectives: 116 us -> 0 us
  Pallas kernels: 0 us -> 69.1 us
  waiting for transfers between devices: 54.1 us -> 0 us
  starting transfers between devices: 42.3 us -> 0 us
  local copies, waits for them, and re-layouts: 16.9 us -> 1.3 us
  other arithmetic: 11.8 us -> 0 us
  between operations: 3.13 us -> 0.01 us
    pallas_call x0 -> x1, Pallas kernels: none -> 69.1 us  [body(): pl.pallas_call(kernel, out_shape=jax.ShapeDtypeStruct((2, vocab), F32), i...]
    all_to_all x5 -> x0, blocking collectives: 67.9 us -> none  [the longest x3 42.3 us: copy_for_each(): return lax.all_to_all(copies, axis, split_axis=0, concat_axis=0, tiled=True)]
    all_to_all x6 -> x0, waiting for transfers between devices: 54.1 us -> none  [the longest x4 35.7 us: copy_for_each(): return lax.all_to_all(copies, axis, split_axis=0, concat_axis=0, tiled=True)]
    all_gather x1 -> x0, blocking collectives: 48.5 us -> none  [one_gather(): lines, at, gathered = (lax.all_gather(vector, axis), 0, [])]
    all_to_all x6 -> x0, starting transfers between devices: 42.3 us -> none  [the longest x4 33.6 us: copy_for_each(): return lax.all_to_all(copies, axis, split_axis=0, concat_axis=0, tiled=True)]
    unnamed x48 -> x1, local copies, waits for them, and re-layouts: 9.05 us -> 1.3 us
    reduce_sum x12 -> x0, other arithmetic: 4.63 us -> none  [the longest x1 1.46 us: body(): squares = taken_together(jnp.sum(resid_in * resid_in, axis=1), 'gy')]
    slice x24 -> x0, local copies, waits for them, and re-layouts: 3.15 us -> none  [the longest x16 1.57 us: folded_in_pairs(): part[side::2]]
  transfers between devices with their start and end apart: 6 -> 0, of which waited for: 6 -> 0; matrix products, arithmetic and copies ran while one was open for 1% -> 0% of each run, Pallas kernels for 0% -> 0%
where the time goes in v1:
time: 70.6 us; the launch traced here: 70.4 us
  Pallas kernels  69.1 us (98%)
  local copies, waits for them, and re-layouts  1.3 us (2%)
    pallas_call x1, Pallas kernels, body(): pl.pallas_call(kernel, out_shape=jax.ShapeDtypeStruct((2, vocab), F32), i...  69.1 us

profile of v1, /device:TPU:1, one launch (start us, length us, event | category | flops | bytes accessed | tf_op | source)
XLA Modules:
  0.0 70.4 jit_solution(2729646566908050448)
XLA Ops:
  0.0 69.1 %shard_map.154 = f32[2,1000]{1,0:T(2,128)} custom-call(s32[2]{0:T(128)} %lengths.1, bf16[1,512]{1,0:T(2,128)(2,1)} %hidden.1, f32[1,512]{1,0:T(1,128)} %bitcast.12, f32[1,512]{1,0:T(1,128)} %bitcast.13, bf16[512,256]{1,0:T(8,128)(2,1)} %query_weight.1, bf16[64,512]{1,0:T(8,128)(2,1)} %bitcast.11, bf16[256,512]{1,0:T(8,128)(2,1)} %out_weight.1, ...), custom_call_target="tpu_custom_call" | custom-call | tf_op jit(solution)/shard_map/pallas_call | solution.py:480
  69.1 1.3 %copy.18 = f32[2,1000]{1,0:T(2,128)} copy(f32[2,1000]{1,0:T(2,128)} %shard_map.154) | data formatting | bytes 16000

commit v2 on v1

v2 whole, which is shorter than its diff:
```python
import functools
import math

import jax
import jax.numpy as jnp
from jax import lax
from jax.experimental import pallas as pl
from jax.experimental.pallas import tpu as pltpu
from jax.sharding import PartitionSpec as P

D = 8192
HEADS = 64
KV_HEADS = 8
HEAD_DIM = 128
D7 = 4096
CTX = 256

EPS = 1e-05
THETA = 10000.0
NEGATIVE = -1e30

GX = 32
GY = 16
NZ = 8
WIDTH = 1024
MESH = pl.DeviceIdType.MESH
BF = jnp.bfloat16
F32 = jnp.float32


def times_transposed(a, b):
    return lax.dot_general(a, b, (((1,), (1,)), ((), ())), preferred_element_type=F32)


def kernel(
    lengths,
    hidden,
    attn_gain,
    final_gain,
    query_weight,
    keyvalue_weight,
    out_weight,
    key_cache,
    value_cache,
    head70,
    adjusted_hidden,
    adjusted_gain,
    adjusted_head,
    base_hidden,
    base_gain,
    base_head,
    out,
    hid_v,
    ag_v,
    fg_v,
    qw_v,
    kvw_v,
    ow_v,
    kv_v,
    h70_v,
    ah_v,
    agn_v,
    ahead_v,
    bh_v,
    bgn_v,
    bhead_v,
    lens_v,
    x_send,
    x_recv,
    st_send,
    st_recv,
    kvw_recv,
    rows_recv,
    cache_recv,
    ab_send,
    ab_recv,
    q_send,
    q_recv,
    kn_send,
    kn_recv,
    e_send,
    e_recv,
    f_send,
    f_recv,
    h_send,
    h_recv,
    abl_send,
    abl_recv,
    i_send,
    i_recv,
    j_send,
    j_recv,
    load_sem,
    send_sem,
    recv_sem,
):
    gx = lax.axis_index("gx")
    gy = lax.axis_index("gy")
    z = gx // 4
    yh = (gx // 2) % 2
    core = gx % 2
    group = gx % 4
    pair = gx - core
    row = 2 * gy + core

    y_lo, x = gy // 4, gy % 4
    plane_y = (3 - y_lo, lax.rem(y_lo + 2, 4), y_lo + 1 - 2 * (y_lo % 2), y_lo)
    plane_x = (lax.rem(x + 2, 4), lax.rem(x + 1, 4), lax.rem(x + 3, 4), x)
    others = [4 * b + a for b in plane_y for a in plane_x][:-1]
    far_z = [lax.rem(z + k, NZ) for k in (4, 3, 5, 2, 6, 1, 7)]

    others_of_group = [lax.rem(group + k, 4) for k in (2, 3, 1)]

    def signal(to):
        pl.semaphore_signal(barrier, inc=1, device_id=to, device_id_type=MESH)

    def over(count, act, first=1):
        lax.fori_loop(first, count, lambda k, c: (act(k), c)[1], 0)

    head_to = (2 * z + yh) % NZ
    block_to = 4 * head_to + 2 * yh + z // 4
    keeps_block = block_to == gx
    projects = yh == z % 2

    pairs = [
        (hidden, hid_v),
        (adjusted_hidden, ah_v),
        (base_hidden, bh_v),
        (adjusted_gain, agn_v),
        (base_gain, bgn_v),
        (attn_gain, ag_v),
        (key_cache, kv_v.at[0]),
        (value_cache, kv_v.at[1]),
        (query_weight, qw_v),
        (keyvalue_weight, kvw_v),
        (out_weight, ow_v),
        (adjusted_head, ahead_v),
        (base_head, bhead_v),
        (final_gain, fg_v),
        (head70, h70_v),
    ]
    loads = [
        pltpu.make_async_copy(src, dst, load_sem.at[n]) for n, (src, dst) in enumerate(pairs)
    ]
    lens_load = pltpu.make_async_copy(lengths, lens_v, load_sem.at[len(pairs) + 2])
    loads[0].start()
    own_cache = [
        pltpu.make_async_copy(
            src.at[:, :, pl.ds(pl.multiple_of(z * HEAD_DIM, HEAD_DIM), HEAD_DIM)],
            rows_recv.at[z, n],
            load_sem.at[len(pairs) + n],
        )
        for n, src in enumerate((key_cache, value_cache))
    ]

    barrier = pltpu.get_barrier_semaphore()
    for g in others_of_group:
        signal((4 * z + g, gy))
    for t in far_z:
        signal((gx + 4 * (t - z), gy))
    for t in others:
        signal((gx, t))
    for half_block in range(2):
        source = 4 * (core * 4 + z // 2) + 2 * yh + half_block

        @pl.when(jnp.logical_and(projects, source != gx))
        def _(source=source):
            signal((source, gy))

    for load in [loads[6], loads[7], loads[9], *own_cache, *loads[1:6], loads[8], lens_load, *loads[10:]]:
        load.start()

    def send(n, src, dst, to):
        pltpu.make_async_remote_copy(
            src_ref=src,
            dst_ref=dst,
            send_sem=send_sem.at[n],
            recv_sem=recv_sem.at[n],
            device_id=to,
            device_id_type=MESH,
        ).start()

    def arrived(n, ref):
        pltpu.make_async_copy(ref, ref, recv_sem.at[n]).wait()

    def sent(n, ref):
        pltpu.make_async_copy(ref, ref, send_sem.at[n]).wait()

    def as_tiles(x, width):
        return [x[:, n * 128 : (n + 1) * 128] for n in range(width // 128)]

    def from_tiles(x):
        return jnp.concatenate([x[:, n, :] for n in range(4)], axis=1)

    loads[0].wait()
    x_send[...] = jnp.concatenate(as_tiles(hid_v[...].astype(F32), 512), axis=0).astype(BF)
    x_recv[z, yh, core] = x_send[...]
    loads[1].wait()
    loads[2].wait()
    adjusted_in = ah_v[...].astype(F32)
    base_in = bh_v[...].astype(F32)
    sum_adjusted = jnp.sum(adjusted_in * adjusted_in, axis=1, keepdims=True)
    sum_base = jnp.sum(base_in * base_in, axis=1, keepdims=True)
    st_send[...] = jnp.concatenate(
        [jnp.broadcast_to(sum_adjusted, (1, 128)), jnp.broadcast_to(sum_base, (1, 128))], axis=0
    )
    st_recv[gy] = st_send[...]
    greeted = NZ - 1 + 3 + GY - 1

    @pl.when(keeps_block)
    def _():
        pl.semaphore_wait(barrier, greeted)

    @pl.when(jnp.logical_not(keeps_block))
    def _():
        pl.semaphore_wait(barrier, greeted + 1)

    def over_group(act):
        for g in others_of_group:
            act(g)

    def over_z(act):
        for t in far_z:
            act(t)

    def head_of(t):
        return pl.ds(pl.multiple_of(t * HEAD_DIM, HEAD_DIM), HEAD_DIM)

    three_tiles = ab_recv.at[pl.ds(0, 3)]
    three_rows = cache_recv.reshape(NZ, 4, 2, 8, HEAD_DIM).at[:, pl.ds(0, 3)]

    over_group(lambda g: send(0, x_send, x_recv.at[z, yh, core], (4 * z + g, gy)))
    loads[9].wait()

    @pl.when(keeps_block)
    def _():
        kvw_recv[core] = kvw_v[...]

    @pl.when(jnp.logical_not(keeps_block))
    def _():
        send(12, kvw_v, kvw_recv.at[core], (block_to, gy))

    loads[6].wait()
    loads[7].wait()
    over_z(
        lambda t: send(2, kv_v.at[:, :, :, head_of(t)], rows_recv.at[z], (gx + 4 * (t - z), gy))
    )
    for t in others:
        send(1, st_send, st_recv.at[gy], (gx, t))
    arrived(0, three_tiles)

    over_z(lambda t: send(13, x_recv.at[z], x_recv.at[z], (gx + 4 * (t - z), gy)))

    def over_gx(act):
        for flip in (1, 0):
            side = 2 * (yh * (1 - flip) + (1 - yh) * flip)
            for to in far_z:
                for c in range(2):
                    act((4 * to + side + c, gy))
        for c in range(2):
            act((4 * z + 2 - 2 * yh + c, gy))
        act((pair + 1 - core, gy))

    arrived(1, st_recv.at[pl.ds(0, GY - 1)])
    totals = jnp.sum(st_recv[...], axis=0)
    loads[3].wait()
    loads[4].wait()
    adjusted = adjusted_in * lax.rsqrt(totals[0:1, 0:1] / D7 + EPS) * agn_v[...]
    base = base_in * lax.rsqrt(totals[1:2, 0:1] / D7 + EPS) * bgn_v[...]
    ab_send[...] = jnp.concatenate(as_tiles(adjusted, 256) + as_tiles(base, 256), axis=0).astype(BF)
    ab_recv[gx] = ab_send[...]
    over_gx(lambda to: send(5, ab_send, ab_recv.at[gx], to))

    for load in own_cache:
        load.wait()
    arrived(2, rows_recv.at[pl.ds(0, NZ - 1)])
    over_group(
        lambda g: send(
            16,
            rows_recv.at[:, :, lax.rem(g, 2)],
            cache_recv.at[:, yh, core],
            (4 * z + g, gy),
        )
    )
    cache_recv[:, yh, core] = rows_recv[:, :, core]

    lane = lax.broadcasted_iota(jnp.int32, (1, HEAD_DIM), 1)
    half = HEAD_DIM // 2
    turn = (lane % half).astype(F32)
    freq = jnp.exp(turn * (-2.0 / HEAD_DIM * math.log(THETA)))
    lens_load.wait()
    length = lens_v[core]
    angle = length.astype(F32) * freq
    cosine = jnp.cos(angle)
    sine = jnp.where(lane < half, -jnp.sin(angle), jnp.sin(angle))

    loads[5].wait()
    loads[8].wait()

    arrived(13, x_recv.at[pl.ds(0, NZ - 1)])
    rows = from_tiles(x_recv[...].astype(F32).reshape(GX, 4, 128))
    squares = jnp.sum(rows * rows, axis=1, keepdims=True)
    scaled = (rows * ag_v[...]).astype(BF)

    @pl.when(projects)
    def _():
        @pl.when(keeps_block)
        def _():
            arrived(12, kvw_recv.at[0])

        @pl.when(jnp.logical_not(keeps_block))
        def _():
            arrived(12, kvw_recv)

        weight = kvw_recv[...].reshape(HEAD_DIM, 512)
        kn_send[...] = times_transposed(scaled, weight).reshape(GX, 1, 128)
        kn_recv[core, gy] = kn_send[row]

        for g in [4 * b + a for b in plane_y[::-1] for a in plane_x]:
            for c in range(2):
                send(15, kn_send.at[2 * g + c], kn_recv.at[core, gy], (4 * z + 2 - 2 * yh + c, g))

    part_q = jnp.dot(scaled, qw_v[...], preferred_element_type=F32)
    high = squares.astype(BF).astype(F32)
    low = squares - high
    pieces = [
        part_q[:, :128],
        part_q[:, 128:],
        jnp.broadcast_to(high, (GX, 128)),
        jnp.broadcast_to(low, (GX, 128)),
    ]
    q_send[...] = jnp.concatenate([p.reshape(GX, 1, 128) for p in pieces], axis=1).astype(BF)
    q_recv[row] = q_send[row]

    def over_plane(act):
        for g in others:
            for c in range(2):
                act(c, 2 * g + c, (pair + c, g))
        act(1 - core, 2 * gy + 1 - core, (pair + 1 - core, gy))

    over_plane(lambda c, r, to: send(3, q_send.at[r], q_recv.at[row], to))

    @pl.when(projects)
    def _():
        over_plane(lambda c, r, to: send(4, kn_send.at[r], kn_recv.at[core, gy], to))

    arrived(5, ab_recv.at[pl.ds(0, GX - 1)])
    joined = from_tiles(ab_recv[...].astype(F32)).astype(BF)
    loads[11].wait()
    loads[12].wait()
    part_ab = times_transposed(joined[:, :256], ahead_v[...]) - times_transposed(
        joined[:, 256:], bhead_v[...]
    )
    vocab = part_ab.shape[1]
    for n in range(GY):
        abl_send[n] = part_ab[2 * n : 2 * n + 2]
    abl_recv[gy] = abl_send[gy]

    arrived(16, three_rows)
    cached = cache_recv[...].reshape(GX, 2, 8, HEAD_DIM).astype(F32)
    keys = cached[:, 0].reshape(CTX, HEAD_DIM).astype(BF)
    values = cached[:, 1].reshape(CTX, HEAD_DIM).astype(BF)

    arrived(3, q_recv.at[pl.ds(0, GX - 1)])
    q_total = jnp.zeros((2, 4, 128), F32)
    for n in range(GY):
        q_total = q_total + q_recv[2 * n : 2 * n + 2].astype(F32)
    square = q_total[0, 2:3, :] + q_total[0, 3:4, :]
    factor = lax.rsqrt(square / D + EPS)
    query = jnp.concatenate([q_total[0, 0:2, :], q_total[1, 0:2, :]], axis=0) * factor
    query = query.astype(BF).astype(F32)
    scale = HEAD_DIM ** (-0.5)
    turned = (query * cosine + pltpu.roll(query, half, 1) * sine).astype(BF)
    scores = times_transposed(turned, keys) * scale
    position = lax.broadcasted_iota(jnp.int32, (4, CTX), 1)
    valid = position < length
    scores = jnp.where(valid, scores, NEGATIVE)
    top = jnp.max(scores, axis=1, keepdims=True)

    @pl.when(projects)
    def _():
        arrived(4, kn_recv.reshape(2 * GY, 1, 128).at[pl.ds(0, 2 * GY - 1)])

    @pl.when(jnp.logical_not(projects))
    def _():
        arrived(15, kn_recv)

    fresh_kv = jnp.sum(kn_recv[...], axis=1)
    key_new = (fresh_kv[0] * factor).astype(BF).astype(F32)
    value_new = (fresh_kv[1] * factor).astype(BF).astype(F32)
    fresh_score = jnp.sum(query * key_new, axis=1, keepdims=True) * scale
    top = jnp.maximum(top, fresh_score)
    weights = jnp.where(valid, jnp.exp(scores - top), 0.0)
    fresh = jnp.exp(fresh_score - top)
    total = jnp.sum(weights, axis=1, keepdims=True) + fresh
    summed = jnp.dot(weights.astype(BF), values, preferred_element_type=F32)
    summed = summed + fresh.astype(BF).astype(F32) * value_new
    attn = (summed / total).astype(BF)
    e_send[0] = attn[0:2]
    e_send[1] = attn[2:4]
    e_recv[row] = e_send[core]

    over_plane(lambda c, r, to: send(6, e_send.at[c], e_recv.at[row], to))

    def to_gy(n, src, dst):
        for t in others:
            send(n, src.at[t], dst.at[gy], (gx, t))

    to_gy(7, abl_send, abl_recv)

    loads[10].wait()
    arrived(6, e_recv.at[pl.ds(0, GX - 1)])
    heads = e_recv[...].astype(F32)
    heads = jnp.concatenate([heads[:, 0, :], heads[:, 1, :]], axis=1).astype(BF)
    mixed = jnp.dot(heads, ow_v[...], preferred_element_type=F32)
    tiles = jnp.concatenate([p.reshape(GX, 1, 128) for p in as_tiles(mixed, 512)], axis=1)
    f_send[...] = tiles.astype(BF).reshape(NZ, 2, 2, 4, 128)
    slot = 2 * z + core
    f_recv[slot] = f_send[z, :, core]

    def over_half(act):
        for to in far_z:
            for c in range(2):
                act(to, c, (4 * to + 2 * yh + c, gy))
        act(z, 1 - core, (pair + 1 - core, gy))

    over_half(lambda d, c, to: send(8, f_send.at[d, :, c], f_recv.at[slot], to))
    arrived(7, abl_recv.at[pl.ds(0, GY - 1)])
    ab_logits = jnp.sum(abl_recv[...], axis=0)
    loads[13].wait()
    loads[14].wait()
    own_rows = x_recv[z, :, core].astype(F32)
    arrived(8, f_recv.at[pl.ds(0, 15)])
    partial = jnp.sum(f_recv[...].astype(F32), axis=0)

    h_send[...] = (partial + own_rows * jnp.where(yh == 0, 1.0, 0.0)).astype(BF)
    h_recv[yh, z, :, core] = h_send[...]
    over_gx(lambda to: send(9, h_send, h_recv.at[yh, z, :, core], to))
    arrived(9, h_recv.reshape(GX, 2, 4, 128).at[pl.ds(0, GX - 1)])
    halves = h_recv[...].astype(F32)
    rows = from_tiles((halves[0] + halves[1]).reshape(GX, 4, 128))
    squares = jnp.sum(rows * rows, axis=1, keepdims=True)
    scaled = (rows * fg_v[...]).astype(BF)
    part = times_transposed(scaled, h70_v[...])
    high = squares.astype(BF).astype(F32)
    low = squares - high
    rest = (WIDTH - vocab) // 2
    tail = [jnp.broadcast_to(high, (GX, rest)), jnp.broadcast_to(low, (GX, rest))]
    part = jnp.concatenate([part, *tail], axis=1).astype(BF)
    for n in range(GY):
        i_send[n] = part[2 * n : 2 * n + 2]
    i_recv[gy] = i_send[gy]

    to_gy(10, i_send, i_recv)
    arrived(10, i_recv.at[pl.ds(0, GY - 1)])
    summed = jnp.sum(i_recv[...].astype(F32), axis=0)
    square = summed[:, vocab : vocab + 1] + summed[:, WIDTH - 1 :]
    factor = lax.rsqrt(square / D + EPS)
    logits = summed[:, :vocab] * factor + ab_logits
    peak = jnp.max(logits, axis=1, keepdims=True)
    partial_lse = peak + jnp.log(jnp.sum(jnp.exp(logits - peak), axis=1, keepdims=True))
    j_send[...] = jnp.broadcast_to(partial_lse, (2, 128))
    j_recv[gx] = j_send[...]

    over_gx(lambda to: send(11, j_send, j_recv.at[gx], to))
    arrived(11, j_recv.at[pl.ds(0, GX - 1)])
    everyone = j_recv[...]
    peak = jnp.max(everyone, axis=0)
    lse = peak + jnp.log(jnp.sum(jnp.exp(everyone - peak[None]), axis=0))
    out[...] = logits - lse[:, 0:1]

    sent(0, three_tiles)
    sent(1, st_recv.at[pl.ds(0, GY - 1)])
    sent(2, rows_recv.at[pl.ds(0, NZ - 1)])
    sent(3, q_recv.at[pl.ds(0, GX - 1)])

    @pl.when(projects)
    def _():
        sent(15, kn_send)
        sent(4, kn_send.at[pl.ds(0, GX - 1)])

    sent(5, ab_recv.at[pl.ds(0, GX - 1)])
    sent(6, e_recv.at[pl.ds(0, GX - 1)])
    sent(7, abl_recv.at[pl.ds(0, GY - 1)])
    sent(8, f_recv.at[pl.ds(0, 15)])
    sent(9, h_recv.reshape(GX, 2, 4, 128).at[pl.ds(0, GX - 1)])
    sent(10, i_recv.at[pl.ds(0, GY - 1)])
    sent(11, j_recv.at[pl.ds(0, GX - 1)])

    @pl.when(jnp.logical_not(keeps_block))
    def _():
        sent(12, kvw_v)

    sent(13, x_recv.at[pl.ds(0, NZ - 1)])
    sent(16, three_rows)


def body(
    hidden70,
    attn_gain,
    final_gain,
    query_weight,
    keyvalue_weight,
    out_weight,
    key_cache,
    value_cache,
    lengths,
    head70,
    adjusted_hidden,
    adjusted_gain,
    adjusted_head,
    base_hidden,
    base_gain,
    base_head,
):
    vocab = head70.shape[1]
    operands = (
        hidden70,
        attn_gain.reshape(1, -1),
        final_gain.reshape(1, -1),
        query_weight,
        keyvalue_weight.T,
        out_weight,
        key_cache,
        value_cache,
        head70.T,
        adjusted_hidden,
        adjusted_gain.reshape(1, -1),
        adjusted_head.T,
        base_hidden,
        base_gain.reshape(1, -1),
        base_head.T,
    )

    def like(a):
        return pltpu.VMEM(a.shape, a.dtype)

    caches = pltpu.VMEM((2, *key_cache.shape), BF)
    local = [like(a) for a in operands[:6]] + [caches] + [like(a) for a in operands[8:]]
    vm = pltpu.VMEM
    exchange = [
        vm((4, 128), BF),
        vm((NZ, 2, 2, 4, 128), BF),
        vm((2, 128), F32),
        vm((GY, 2, 128), F32),
        vm((2, 64, 512), BF),
        vm((NZ, 2, 2, 8, HEAD_DIM), BF),
        vm((NZ, 2, 2, 2, 8, 128), BF),
        vm((4, 128), BF),
        vm((GX, 4, 128), BF),
        vm((GX, 4, 128), BF),
        vm((GX, 4, 128), BF),
        vm((GX, 1, 128), F32),
        vm((2, GY, 1, 128), F32),
        vm((2, 2, 128), BF),
        vm((GX, 2, 128), BF),
        vm((NZ, 2, 2, 4, 128), BF),
        vm((16, 2, 4, 128), BF),
        vm((2, 4, 128), BF),
        vm((2, NZ, 2, 2, 4, 128), BF),
        vm((GY, 2, vocab), F32),
        vm((GY, 2, vocab), F32),
        vm((GY, 2, WIDTH), BF),
        vm((GY, 2, WIDTH), BF),
        vm((2, 128), F32),
        vm((GX, 2, 128), F32),
    ]
    return pl.pallas_call(
        kernel,
        out_shape=pltpu.VMEM((2, vocab), F32),
        in_specs=[pl.BlockSpec(memory_space=pl.ANY)] * (1 + len(operands)),
        out_specs=pl.BlockSpec(memory_space=pltpu.VMEM),
        scratch_shapes=local
        + [pltpu.SMEM(lengths.shape, lengths.dtype)]
        + exchange
        + [
            pltpu.SemaphoreType.DMA((18,)),
            pltpu.SemaphoreType.DMA((17,)),
            pltpu.SemaphoreType.DMA((17,)),
        ],
        compiler_params=pltpu.CompilerParams(collective_id=0, has_side_effects=True),
    )(lengths, *operands)


def solution(mesh):
    placed = (
        P("gx", "gy"),
        P("gy"),
        P("gy"),
        P("gy", "gx"),
        P("gy", "gx"),
        P("gx", "gy"),
        P("gy", "gx", None),
        P("gy", "gx", None),
        P("gy"),
        P("gy", "gx"),
        P("gx", "gy"),
        P("gy"),
        P("gy", "gx"),
        P("gx", "gy"),
        P("gy"),
        P("gy", "gx"),
    )
    return jax.shard_map(body, mesh=mesh, in_specs=placed, out_specs=P("gy", "gx"), check_vma=False)
```

time: 70.6 us -> 61.1 us (0.87)
  Pallas kernels: 69.1 us -> 60.3 us
    pallas_call x1, Pallas kernels: 69.1 us -> 60.3 us  [body(): pl.pallas_call(kernel, out_shape=pltpu.VMEM((2, vocab), F32), in_specs=[p...]
where the time goes in v2:
time: 61.1 us; the launch traced here: 60.9 us
  Pallas kernels  60.3 us (99%)
    pallas_call x1, Pallas kernels, body(): pl.pallas_call(kernel, out_shape=pltpu.VMEM((2, vocab), F32), in_specs=[p...  60.3 us

profile of v2, /device:TPU:1, one launch (start us, length us, event | category | flops | bytes accessed | tf_op | source)
XLA Modules:
  0.0 60.9 jit_solution(1771337369867395565)
XLA Ops:
  0.0 60.3 %shard_map.154 = f32[2,1000]{1,0:T(2,128)S(1)} custom-call(s32[2]{0:T(128)} %lengths.1, bf16[1,512]{1,0:T(2,128)(2,1)} %hidden.1, f32[1,512]{1,0:T(1,128)} %bitcast.12, f32[1,512]{1,0:T(1,128)} %bitcast.13, bf16[512,256]{1,0:T(8,128)(2,1)} %query_weight.1, bf16[64,512]{1,0:T(8,128)(2,1)} %bitcast.11, bf16[256,512]{1,0:T(8,128)(2,1)} %out_weight.1, ...), custom_call_target="tpu_custom_call" | custom-call | tf_op jit(solution)/shard_map/pallas_call | solution.py:568
  60.3 0.6 copy.18

commit v3 on v2

--- a/solution.py
+++ b/solution.py
@@ -201,9 +201,10 @@
     base_in = bh_v[...].astype(F32)
     sum_adjusted = jnp.sum(adjusted_in * adjusted_in, axis=1, keepdims=True)
     sum_base = jnp.sum(base_in * base_in, axis=1, keepdims=True)
-    st_send[...] = jnp.concatenate(
-        [jnp.broadcast_to(sum_adjusted, (1, 128)), jnp.broadcast_to(sum_base, (1, 128))], axis=0
-    )
+    hidden_in = hid_v[...].astype(F32)
+    sum_hidden = jnp.sum(hidden_in * hidden_in, axis=1, keepdims=True)
+    sums = (sum_adjusted, sum_base, sum_hidden, sum_hidden)
+    st_send[...] = jnp.concatenate([jnp.broadcast_to(t, (1, 128)) for t in sums], axis=0)
     st_recv[gy] = st_send[...]
     greeted = NZ - 1 + 3 + GY - 1
 
@@ -226,25 +227,25 @@
     def head_of(t):
         return pl.ds(pl.multiple_of(t * HEAD_DIM, HEAD_DIM), HEAD_DIM)
 
-    three_tiles = ab_recv.at[pl.ds(0, 3)]
+    three_tiles = x_recv.reshape(GX, 4, 128).at[pl.ds(0, 3)]
     three_rows = cache_recv.reshape(NZ, 4, 2, 8, HEAD_DIM).at[:, pl.ds(0, 3)]
 
     over_group(lambda g: send(0, x_send, x_recv.at[z, yh, core], (4 * z + g, gy)))
-    loads[9].wait()
-
-    @pl.when(keeps_block)
-    def _():
-        kvw_recv[core] = kvw_v[...]
-
-    @pl.when(jnp.logical_not(keeps_block))
-    def _():
-        send(12, kvw_v, kvw_recv.at[core], (block_to, gy))
-
     loads[6].wait()
     loads[7].wait()
     over_z(
         lambda t: send(2, kv_v.at[:, :, :, head_of(t)], rows_recv.at[z], (gx + 4 * (t - z), gy))
     )
+    loads[9].wait()
+
+    @pl.when(keeps_block)
+    def _():
+        kvw_recv[core] = kvw_v[...]
+
+    @pl.when(jnp.logical_not(keeps_block))
+    def _():
+        send(12, kvw_v, kvw_recv.at[core], (block_to, gy))
+
     for t in others:
         send(1, st_send, st_recv.at[gy], (gx, t))
     arrived(0, three_tiles)
@@ -267,7 +268,11 @@
     loads[4].wait()
     adjusted = adjusted_in * lax.rsqrt(totals[0:1, 0:1] / D7 + EPS) * agn_v[...]
     base = base_in * lax.rsqrt(totals[1:2, 0:1] / D7 + EPS) * bgn_v[...]
-    ab_send[...] = jnp.concatenate(as_tiles(adjusted, 256) + as_tiles(base, 256), axis=0).astype(BF)
+    factor = lax.rsqrt(totals[2:3, :] / D + EPS)
+    high = factor.astype(BF).astype(F32)
+    ab_send[...] = jnp.concatenate(
+        as_tiles(adjusted, 256) + as_tiles(base, 256) + [high, factor - high], axis=0
+    ).astype(BF)
     ab_recv[gx] = ab_send[...]
     over_gx(lambda to: send(5, ab_send, ab_recv.at[gx], to))
 
@@ -299,7 +304,6 @@
 
     arrived(13, x_recv.at[pl.ds(0, NZ - 1)])
     rows = from_tiles(x_recv[...].astype(F32).reshape(GX, 4, 128))
-    squares = jnp.sum(rows * rows, axis=1, keepdims=True)
     scaled = (rows * ag_v[...]).astype(BF)
 
     @pl.when(projects)
@@ -321,15 +325,9 @@
                 send(15, kn_send.at[2 * g + c], kn_recv.at[core, gy], (4 * z + 2 - 2 * yh + c, g))
 
     part_q = jnp.dot(scaled, qw_v[...], preferred_element_type=F32)
-    high = squares.astype(BF).astype(F32)
-    low = squares - high
-    pieces = [
-        part_q[:, :128],
-        part_q[:, 128:],
-        jnp.broadcast_to(high, (GX, 128)),
-        jnp.broadcast_to(low, (GX, 128)),
-    ]
-    q_send[...] = jnp.concatenate([p.reshape(GX, 1, 128) for p in pieces], axis=1).astype(BF)
+    q_send[...] = jnp.concatenate(
+        [p.reshape(GX, 1, 128) for p in as_tiles(part_q, 256)], axis=1
+    ).astype(BF)
     q_recv[row] = q_send[row]
 
     def over_plane(act):
@@ -355,6 +353,8 @@
     for n in range(GY):
         abl_send[n] = part_ab[2 * n : 2 * n + 2]
     abl_recv[gy] = abl_send[gy]
+    parts = ab_recv[row].astype(F32)
+    factor = parts[4:5, :] + parts[5:6, :]
 
     arrived(16, three_rows)
     cached = cache_recv[...].reshape(GX, 2, 8, HEAD_DIM).astype(F32)
@@ -362,12 +362,10 @@
     values = cached[:, 1].reshape(CTX, HEAD_DIM).astype(BF)
 
     arrived(3, q_recv.at[pl.ds(0, GX - 1)])
-    q_total = jnp.zeros((2, 4, 128), F32)
+    q_total = jnp.zeros((2, 2, 128), F32)
     for n in range(GY):
         q_total = q_total + q_recv[2 * n : 2 * n + 2].astype(F32)
-    square = q_total[0, 2:3, :] + q_total[0, 3:4, :]
-    factor = lax.rsqrt(square / D + EPS)
-    query = jnp.concatenate([q_total[0, 0:2, :], q_total[1, 0:2, :]], axis=0) * factor
+    query = jnp.concatenate([q_total[0], q_total[1]], axis=0) * factor
     query = query.astype(BF).astype(F32)
     scale = HEAD_DIM ** (-0.5)
     turned = (query * cosine + pltpu.roll(query, half, 1) * sine).astype(BF)
@@ -406,7 +404,6 @@
         for t in others:
             send(n, src.at[t], dst.at[gy], (gx, t))
 
-    to_gy(7, abl_send, abl_recv)
 
     loads[10].wait()
     arrived(6, e_recv.at[pl.ds(0, GX - 1)])
@@ -425,8 +422,7 @@
         act(z, 1 - core, (pair + 1 - core, gy))
 
     over_half(lambda d, c, to: send(8, f_send.at[d, :, c], f_recv.at[slot], to))
-    arrived(7, abl_recv.at[pl.ds(0, GY - 1)])
-    ab_logits = jnp.sum(abl_recv[...], axis=0)
+    to_gy(7, abl_send, abl_recv)
     loads[13].wait()
     loads[14].wait()
     own_rows = x_recv[z, :, core].astype(F32)
@@ -436,6 +432,8 @@
     h_send[...] = (partial + own_rows * jnp.where(yh == 0, 1.0, 0.0)).astype(BF)
     h_recv[yh, z, :, core] = h_send[...]
     over_gx(lambda to: send(9, h_send, h_recv.at[yh, z, :, core], to))
+    arrived(7, abl_recv.at[pl.ds(0, GY - 1)])
+    ab_logits = jnp.sum(abl_recv[...], axis=0)
     arrived(9, h_recv.reshape(GX, 2, 4, 128).at[pl.ds(0, GX - 1)])
     halves = h_recv[...].astype(F32)
     rows = from_tiles((halves[0] + halves[1]).reshape(GX, 4, 128))
@@ -541,15 +539,15 @@
     exchange = [
         vm((4, 128), BF),
         vm((NZ, 2, 2, 4, 128), BF),
-        vm((2, 128), F32),
-        vm((GY, 2, 128), F32),
+        vm((4, 128), F32),
+        vm((GY, 4, 128), F32),
         vm((2, 64, 512), BF),
         vm((NZ, 2, 2, 8, HEAD_DIM), BF),
         vm((NZ, 2, 2, 2, 8, 128), BF),
-        vm((4, 128), BF),
-        vm((GX, 4, 128), BF),
-        vm((GX, 4, 128), BF),
-        vm((GX, 4, 128), BF),
+        vm((6, 128), BF),
+        vm((GX, 6, 128), BF),
+        vm((GX, 2, 128), BF),
+        vm((GX, 2, 128), BF),
         vm((GX, 1, 128), F32),
         vm((2, GY, 1, 128), F32),
         vm((2, 2, 128), BF),

time: 61.1 us -> 60.8 us (level)
  no operation moved by 1% of the time
where the time goes in v3:
time: 60.8 us; the launch traced here: 60.7 us
  Pallas kernels  60.1 us (99%)
    pallas_call x1, Pallas kernels, body(): pl.pallas_call(kernel, out_shape=pltpu.VMEM((2, vocab), F32), in_specs=[p...  60.1 us

profile of v3, /device:TPU:1, one launch (start us, length us, event | category | flops | bytes accessed | tf_op | source)
XLA Modules:
  0.0 60.7 jit_solution(2450146177668392413)
XLA Ops:
  0.0 60.1 %shard_map.154 = f32[2,1000]{1,0:T(2,128)S(1)} custom-call(s32[2]{0:T(128)} %lengths.1, bf16[1,512]{1,0:T(2,128)(2,1)} %hidden.1, f32[1,512]{1,0:T(1,128)} %bitcast.12, f32[1,512]{1,0:T(1,128)} %bitcast.13, bf16[512,256]{1,0:T(8,128)(2,1)} %query_weight.1, bf16[64,512]{1,0:T(8,128)(2,1)} %bitcast.11, bf16[256,512]{1,0:T(8,128)(2,1)} %out_weight.1, ...), custom_call_target="tpu_custom_call" | custom-call | tf_op jit(solution)/shard_map/pallas_call | solution.py:566
  60.1 0.6 copy.18

commit v4 on v3

--- a/solution.py
+++ b/solution.py
@@ -154,10 +154,10 @@
     ]
 
     barrier = pltpu.get_barrier_semaphore()
+    for t in far_z:
+        signal((gx + 4 * (t - z), gy))
     for g in others_of_group:
         signal((4 * z + g, gy))
-    for t in far_z:
-        signal((gx + 4 * (t - z), gy))
     for t in others:
         signal((gx, t))
     for half_block in range(2):
@@ -195,6 +195,31 @@
     loads[0].wait()
     x_send[...] = jnp.concatenate(as_tiles(hid_v[...].astype(F32), 512), axis=0).astype(BF)
     x_recv[z, yh, core] = x_send[...]
+    greeted = NZ - 1 + 3 + GY - 1
+
+    @pl.when(keeps_block)
+    def _():
+        pl.semaphore_wait(barrier, greeted)
+
+    @pl.when(jnp.logical_not(keeps_block))
+    def _():
+        pl.semaphore_wait(barrier, greeted + 1)
+
+    def over_group(act):
+        for g in others_of_group:
+            act(g)
+
+    def over_z(act):
+        for t in far_z:
+            act(t)
+
+    def head_of(t):
+        return pl.ds(pl.multiple_of(t * HEAD_DIM, HEAD_DIM), HEAD_DIM)
+
+    three_tiles = x_recv.reshape(GX, 4, 128).at[pl.ds(0, 3)]
+    three_rows = cache_recv.reshape(NZ, 4, 2, 8, HEAD_DIM).at[:, pl.ds(0, 3)]
+
+    over_group(lambda g: send(0, x_send, x_recv.at[z, yh, core], (4 * z + g, gy)))
     loads[1].wait()
     loads[2].wait()
     adjusted_in = ah_v[...].astype(F32)
@@ -206,31 +231,9 @@
     sums = (sum_adjusted, sum_base, sum_hidden, sum_hidden)
     st_send[...] = jnp.concatenate([jnp.broadcast_to(t, (1, 128)) for t in sums], axis=0)
     st_recv[gy] = st_send[...]
-    greeted = NZ - 1 + 3 + GY - 1
-
-    @pl.when(keeps_block)
-    def _():
-        pl.semaphore_wait(barrier, greeted)
-
-    @pl.when(jnp.logical_not(keeps_block))
-    def _():
-        pl.semaphore_wait(barrier, greeted + 1)
-
-    def over_group(act):
-        for g in others_of_group:
-            act(g)
-
-    def over_z(act):
-        for t in far_z:
-            act(t)
-
-    def head_of(t):
-        return pl.ds(pl.multiple_of(t * HEAD_DIM, HEAD_DIM), HEAD_DIM)
-
-    three_tiles = x_recv.reshape(GX, 4, 128).at[pl.ds(0, 3)]
-    three_rows = cache_recv.reshape(NZ, 4, 2, 8, HEAD_DIM).at[:, pl.ds(0, 3)]
-
-    over_group(lambda g: send(0, x_send, x_recv.at[z, yh, core], (4 * z + g, gy)))
+    for t in others:
+        send(1, st_send, st_recv.at[gy], (gx, t))
+
     loads[6].wait()
     loads[7].wait()
     over_z(
@@ -246,8 +249,6 @@
     def _():
         send(12, kvw_v, kvw_recv.at[core], (block_to, gy))
 
-    for t in others:
-        send(1, st_send, st_recv.at[gy], (gx, t))
     arrived(0, three_tiles)
 
     over_z(lambda t: send(13, x_recv.at[z], x_recv.at[z], (gx + 4 * (t - z), gy)))
@@ -411,32 +412,32 @@
     heads = jnp.concatenate([heads[:, 0, :], heads[:, 1, :]], axis=1).astype(BF)
     mixed = jnp.dot(heads, ow_v[...], preferred_element_type=F32)
     tiles = jnp.concatenate([p.reshape(GX, 1, 128) for p in as_tiles(mixed, 512)], axis=1)
-    f_send[...] = tiles.astype(BF).reshape(NZ, 2, 2, 4, 128)
-    slot = 2 * z + core
-    f_recv[slot] = f_send[z, :, core]
-
-    def over_half(act):
-        for to in far_z:
-            for c in range(2):
-                act(to, c, (4 * to + 2 * yh + c, gy))
-        act(z, 1 - core, (pair + 1 - core, gy))
-
-    over_half(lambda d, c, to: send(8, f_send.at[d, :, c], f_recv.at[slot], to))
+    f_send[...] = tiles.astype(BF).reshape(2, 4, 2, 2, 4, 128)
+    z_half, z_in = z // 4, z % 4
+    slot = 2 * z_in + core
+    f_recv[slot] = f_send[:, z_in, :, core]
+
+    for to in (3 - z_in, lax.rem(z_in + 2, 4), z_in + 1 - 2 * (z_in % 2)):
+        for c in range(2):
+            there = (4 * (4 * z_half + to) + 2 * yh + c, gy)
+            send(8, f_send.at[:, to, :, c], f_recv.at[slot], there)
+    send(8, f_send.at[:, z_in, :, 1 - core], f_recv.at[slot], (pair + 1 - core, gy))
     to_gy(7, abl_send, abl_recv)
     loads[13].wait()
     loads[14].wait()
-    own_rows = x_recv[z, :, core].astype(F32)
-    arrived(8, f_recv.at[pl.ds(0, 15)])
+    own_rows = x_recv.reshape(2, 4, 2, 2, 4, 128)[:, z_in, :, core].astype(F32)
+    quarter = 2 * z_half + yh
+    own_rows = own_rows * jnp.where(quarter == 0, 1.0, 0.0)
+    arrived(8, f_recv.at[pl.ds(0, 7)])
     partial = jnp.sum(f_recv[...].astype(F32), axis=0)
 
-    h_send[...] = (partial + own_rows * jnp.where(yh == 0, 1.0, 0.0)).astype(BF)
-    h_recv[yh, z, :, core] = h_send[...]
-    over_gx(lambda to: send(9, h_send, h_recv.at[yh, z, :, core], to))
+    h_send[...] = (partial + own_rows).astype(BF)
+    h_recv[quarter, :, z_in, :, core] = h_send[...]
+    over_gx(lambda to: send(9, h_send, h_recv.at[quarter, :, z_in, :, core], to))
     arrived(7, abl_recv.at[pl.ds(0, GY - 1)])
     ab_logits = jnp.sum(abl_recv[...], axis=0)
-    arrived(9, h_recv.reshape(GX, 2, 4, 128).at[pl.ds(0, GX - 1)])
-    halves = h_recv[...].astype(F32)
-    rows = from_tiles((halves[0] + halves[1]).reshape(GX, 4, 128))
+    arrived(9, h_recv.reshape(GX, 4, 4, 128).at[pl.ds(0, GX - 1)])
+    rows = from_tiles(jnp.sum(h_recv[...].astype(F32), axis=0).reshape(GX, 4, 128))
     squares = jnp.sum(rows * rows, axis=1, keepdims=True)
     scaled = (rows * fg_v[...]).astype(BF)
     part = times_transposed(scaled, h70_v[...])
@@ -480,8 +481,8 @@
     sent(5, ab_recv.at[pl.ds(0, GX - 1)])
     sent(6, e_recv.at[pl.ds(0, GX - 1)])
     sent(7, abl_recv.at[pl.ds(0, GY - 1)])
-    sent(8, f_recv.at[pl.ds(0, 15)])
-    sent(9, h_recv.reshape(GX, 2, 4, 128).at[pl.ds(0, GX - 1)])
+    sent(8, f_recv.at[pl.ds(0, 7)])
+    sent(9, h_recv.reshape(GX, 4, 4, 128).at[pl.ds(0, GX - 1)])
     sent(10, i_recv.at[pl.ds(0, GY - 1)])
     sent(11, j_recv.at[pl.ds(0, GX - 1)])
 
@@ -552,10 +553,10 @@
         vm((2, GY, 1, 128), F32),
         vm((2, 2, 128), BF),
         vm((GX, 2, 128), BF),
-        vm((NZ, 2, 2, 4, 128), BF),
-        vm((16, 2, 4, 128), BF),
-        vm((2, 4, 128), BF),
-        vm((2, NZ, 2, 2, 4, 128), BF),
+        vm((2, 4, 2, 2, 4, 128), BF),
+        vm((8, 2, 2, 4, 128), BF),
+        vm((2, 2, 4, 128), BF),
+        vm((4, 2, 4, 2, 2, 4, 128), BF),
         vm((GY, 2, vocab), F32),
         vm((GY, 2, vocab), F32),
         vm((GY, 2, WIDTH), BF),

time: 60.8 us -> 61.1 us (level)
  no operation moved by 1% of the time
where the time goes in v4:
time: 61.1 us; the launch traced here: 61 us
  Pallas kernels  60.4 us (99%)
    pallas_call x1, Pallas kernels, body(): pl.pallas_call(kernel, out_shape=pltpu.VMEM((2, vocab), F32), in_specs=[p...  60.4 us

profile of v4, /device:TPU:1, one launch (start us, length us, event | category | flops | bytes accessed | tf_op | source)
XLA Modules:
  0.0 61.0 jit_solution(1221299471803598145)
XLA Ops:
  0.0 60.4 %shard_map.154 = f32[2,1000]{1,0:T(2,128)S(1)} custom-call(s32[2]{0:T(128)} %lengths.1, bf16[1,512]{1,0:T(2,128)(2,1)} %hidden.1, f32[1,512]{1,0:T(1,128)} %bitcast.12, f32[1,512]{1,0:T(1,128)} %bitcast.13, bf16[512,256]{1,0:T(8,128)(2,1)} %query_weight.1, bf16[64,512]{1,0:T(8,128)(2,1)} %bitcast.11, bf16[256,512]{1,0:T(8,128)(2,1)} %out_weight.1, ...), custom_call_target="tpu_custom_call" | custom-call | tf_op jit(solution)/shard_map/pallas_call | solution.py:567
  60.4 0.6 copy.18
